TPU v7x, 32 devices: a whole 2x2x4 slice. The times are simulated.
32 devices in a mesh: dp: 8 (over z, x), mp: 4 (over y, core).
Axes of the slice: x: 2, y: 2, z: 4, core: 2. Of those that a mesh axis runs over, the one named last changes fastest.
Arguments:
- tokens: bfloat16 [1024, 4096], P('dp'), may hold values from -6 to 6
- cotangent: bfloat16 [1024, 4096], P('dp', 'mp'), may hold values from -6 to 6
- sketch: float32 [4096, 128], P('dp'), may hold values from -12 to 12
Outputs:
- precond: bfloat16 [4096, 4096], P('dp', 'mp')
- new_sketch: float32 [4096, 128], P('dp')
All inputs are finite; a program needn't handle non-finite values.
Results may differ from a plain program's by a relative error of at most 0.001.
Values sent between devices are 32-bit elements; how exact they have to be, the bound alone decides.
A program may use at most 64 MiB of HBM per device.

v0:
```python
import math
import jax
import jax.numpy as jnp
from jax import lax
from jax.sharding import PartitionSpec as P

DECAY_RATE = 0.9
RIDGE_FRAC = 0.0001


def product(left_mat, right_mat):
    return jnp.dot(left_mat, right_mat, precision=lax.Precision.HIGHEST)


def right_solve(values, lower_tri):
    return lax.linalg.triangular_solve(
        lower_tri, values, left_side=False, lower=True, transpose_a=True
    )


def left_solve(lower_tri, values, transpose):
    return lax.linalg.triangular_solve(
        lower_tri, values, left_side=True, lower=True, transpose_a=transpose
    )


def spd_solve(matrix, target):
    lower_tri = jnp.linalg.cholesky(matrix)
    return left_solve(lower_tri, left_solve(lower_tri, target, False), True)


def shards(tokens, cotangent, sketch):
    dp_count = lax.axis_size("dp")
    rank_size = sketch.shape[1]
    norm_scale = 1.0 / math.sqrt(tokens.shape[0] * dp_count)
    gradient = lax.psum_scatter(
        lax.dot_general(
            tokens, cotangent, (((0,), (0,)), ((), ())), preferred_element_type=jnp.float32
        )
        * norm_scale,
        "dp",
        scatter_dimension=0,
        tiled=True,
    )
    identity = jnp.eye(rank_size, dtype=jnp.float32)

    def covariance(sketch_proj, grad_proj):
        partial_cols = product(gradient, grad_proj)
        summed = lax.psum(partial_cols, "mp")
        return DECAY_RATE * product(sketch, sketch_proj) + summed

    sketch_proj, grad_proj = lax.psum(
        (product(sketch.T, sketch), product(gradient.T, sketch)), "dp"
    )
    applied = covariance(sketch_proj, grad_proj)
    gram_mat, sketch_image, grad_image = lax.psum(
        (product(applied.T, applied), product(sketch.T, applied), product(gradient.T, applied)),
        "dp",
    )
    previous_low = jnp.linalg.cholesky(gram_mat)
    previous = applied
    applied = covariance(
        right_solve(sketch_image, previous_low), right_solve(grad_image, previous_low)
    )
    cross_prev, self_image, image_grad = lax.psum(
        (product(previous.T, applied), product(applied.T, applied), product(applied.T, gradient)),
        "dp",
    )
    rayleigh = left_solve(previous_low, cross_prev, False)
    rayleigh = 0.5 * (rayleigh + rayleigh.T)
    mean_level = jnp.trace(rayleigh) / rank_size
    new_low = jnp.linalg.cholesky(rayleigh + RIDGE_FRAC * mean_level * identity)
    new_sketch = right_solve(applied, new_low)
    self_gram = right_solve(left_solve(new_low, self_image, False), new_low)
    cross_mat = left_solve(new_low, image_grad, False)
    inner_mat = mean_level * identity + self_gram
    precond = gradient - product(new_sketch, spd_solve(inner_mat, cross_mat))
    return (precond.astype(jnp.bfloat16), new_sketch)


def solution(mesh):
    in_specs = (P("dp", None), P("dp", "mp"), P("dp", None))
    out_specs = (P("dp", "mp"), P("dp", None))
    return jax.shard_map(shards, mesh=mesh, in_specs=in_specs, out_specs=out_specs, check_vma=False)
```

profile of v0, /device:TPU:0, one launch (start us, length us, event | category | flops | bytes accessed | tf_op | source)
XLA Modules:
  0.0 714.0 jit_solution(3880884214434900595)
XLA Ops:
  7.2 1.2 copy-done
  8.4 9.0 %convolution_multiply_fusion = f32[4096,1024]{1,0:T(8,128)} fusion(bf16[128,4096]{1,0:T(8,128)(2,1)S(1)} %copy-done, bf16[128,1024]{1,0:T(8,128)(2,1)} %param.11), kind=kOutput, calls=%fused_computation | convolution fusion | flops 1077936128 | bytes 18087936 | tf_op jit(solution)/shard_map/dot_general | solution.py:37
  17.5 0.9 copy-done.2
  18.4 1.2 fusion.33
  19.6 280.3 %reduce-scatter.2.cloned.1.call-done = f32[512,1024]{1,0:T(8,128)} async-done(((f32[4096,1024]{1,0:T(8,128)}), f32[512,1024]{1,0:T(8,128)}) %reduce-scatter.2.cloned.1.call-update) | async-done | bytes 2097168 | tf_op jit(solution)/shard_map/reduce_scatter | solution.py:36
  299.9 6.0 fusion.34
  305.9 72.5 %all-reduce.17.cloned.1.call-done = (f32[1024,128]{1,0:T(8,128)}, f32[128,128]{1,0:T(8,128)}) async-done(((f32[1024,128]{1,0:T(8,128)}, f32[128,128]{1,0:T(8,128)}), (f32[1024,128]{1,0:T(8,128)}, f32[128,128]{1,0:T(8,128)})) %all-reduce.17.cloned.1.call-update) | async-done | bytes 589840 | tf_op jit(solution)/shard_map/psum | solution.py:52
  378.4 4.1 fusion.35
  383.0 31.1 %all-reduce.9.cloned.1.call-done = f32[512,128]{0,1:T(8,128)} async-done(((f32[512,128]{0,1:T(8,128)}), f32[512,128]{0,1:T(8,128)}) %all-reduce.9.cloned.1.call-update) | async-done | bytes 262160 | tf_op jit(solution)/shard_map/psum | solution.py:49
  414.1 1.4 fusion.3
  415.5 1.0 convolution_bitcast_fusion.2
  416.5 1.0 fusion.36
  417.5 4.2 fusion.37
  421.8 74.2 %all-reduce.15.cloned.1.call-done = (f32[1024,128]{1,0:T(8,128)}, f32[128,128]{0,1:T(8,128)}, f32[128,128]{0,1:T(8,128)}) async-done(((f32[1024,128]{1,0:T(8,128)}, f32[128,128]{0,1:T(8,128)}, f32[128,128]{0,1:T(8,128)}), (f32[1024,128]{1,0:T(8,128)}, f32[128,128]{0,1:T(8,128)}, f32[128,128]{0,1:T(8,128)})) %all-reduce.15.cloned.1.call-update) | async-done | bytes 655376 | tf_op jit(solution)/shard_map/psum | solution.py:56
  496.0 0.9 copy.7
  496.9 0.9 fusion.27
  497.8 11.7 %cholesky.59 = f32[128,128]{1,0:T(8,128)S(1)} custom-call(f32[128,128]{1,0:T(8,128)S(1)} %fusion.27), custom_call_target="Cholesky" | custom-call | tf_op jit(solution)/shard_map/jit(cholesky)/cholesky | solution.py:60
  510.2 0.7 fusion.5
  510.8 9.8 %custom-call.26 = f32[1,128,128]{1,2,0:T(8,128)S(1)} custom-call(f32[1,128,128]{2,1,0:T(8,128)S(1)} %fusion.5), custom_call_target="InvertDiagBlocksLowerTriangular" | custom-call | tf_op jit(solution)/shard_map/triangular_solve/custom-call.0 | solution.py:16
  520.7 1.6 fusion.24
  522.3 3.0 fusion.38
  525.5 1.1 convolution_bitcast_fusion.1
  526.6 30.5 %all-reduce.11.cloned.1.call-done = f32[512,128]{0,1:T(8,128)} async-done(((f32[512,128]{0,1:T(8,128)}), f32[512,128]{0,1:T(8,128)}) %all-reduce.11.cloned.1.call-update) | async-done | bytes 262160 | tf_op jit(solution)/shard_map/psum | solution.py:49
  557.1 1.3 fusion.1
  558.5 2.0 fusion.39
  560.5 1.0 fusion.40
  561.5 2.1 fusion.41
  563.6 74.3 %all-reduce.13.cloned.1.call-done = (f32[128,128]{1,0:T(8,128)}, f32[128,1024]{1,0:T(8,128)}, f32[128,128]{1,0:T(8,128)}) async-done(((f32[128,128]{1,0:T(8,128)}, f32[128,1024]{1,0:T(8,128)}, f32[128,128]{1,0:T(8,128)}), (f32[128,128]{1,0:T(8,128)}, f32[128,1024]{1,0:T(8,128)}, f32[128,128]{1,0:T(8,128)})) %all-reduce.13.cloned.1.call-update) | async-done | bytes 655376 | tf_op jit(solution)/shard_map/psum | solution.py:65
  637.9 1.1 fusion.22
  640.4 0.9 fusion.32
  641.2 0.7 copy.10
  642.0 0.8 fusion.20
  642.8 0.7 copy.11
  643.5 12.5 %cholesky.70 = f32[128,128]{1,0:T(8,128)S(1)} custom-call(f32[128,128]{1,0:T(8,128)} %copy.11), custom_call_target="Cholesky" | custom-call | tf_op jit(solution)/shard_map/jit(cholesky)/cholesky | solution.py:72
  656.8 0.7 fusion.6
  657.4 9.8 %custom-call.21 = f32[1,128,128]{1,2,0:T(8,128)S(1)} custom-call(f32[1,128,128]{2,1,0:T(8,128)S(1)} %fusion.6), custom_call_target="InvertDiagBlocksLowerTriangular" | custom-call | tf_op jit(solution)/shard_map/triangular_solve | solution.py:16
  667.3 1.3 fusion.18
  668.5 1.8 fusion.15
  670.9 1.1 fusion.4
  672.0 0.7 copy.13
  672.7 1.5 fusion.12
  674.2 1.6 copy.14
  675.7 12.7 %cholesky.81 = f32[128,128]{1,0:T(8,128)S(1)} custom-call(f32[128,128]{1,0:T(8,128)} %copy.14), custom_call_target="Cholesky" | custom-call | tf_op jit(solution)/shard_map/jit(cholesky)/cholesky | solution.py:28
  688.5 0.7 compare_reduce_fusion
  689.2 1.3 fusion.7
  690.6 10.6 %custom-call.22 = f32[1,128,128]{1,2,0:T(8,128)S(1)} custom-call(f32[1,128,128]{2,1,0:T(8,128)} %fusion.7), custom_call_target="InvertDiagBlocksLowerTriangular" | custom-call | tf_op jit(solution)/shard_map/triangular_solve | solution.py:22
  701.2 1.7 fusion.13
  704.1 2.8 subtract_convert_fusion
  (37 shorter events, 4.3 us)
Async XLA Ops:
  7.2 1.2 copy-start
  7.2 292.7 %reduce-scatter.2.cloned.1.call-start = ((), (), s32[]{:S(2)}) async-start(), calls=%async_computation.1 | async-start | bytes 18874368 | tf_op jit(solution)/shard_map/reduce_scatter | solution.py:36
  17.4 0.9 copy-start.2
  17.5 361.0 %all-reduce.17.cloned.1.call-start = ((), (), s32[]{:S(2)}) async-start(), calls=%async_computation.6 | async-start | bytes 1179648 | tf_op jit(solution)/shard_map/psum | solution.py:52
  299.9 78.6 %copy-start.1 = (f32[512,1024]{1,0:T(8,128)S(1)}, f32[512,1024]{1,0:T(8,128)}, u32[]{:S(2)}) copy-start(f32[512,1024]{1,0:T(8,128)} %reduce-scatter.2.cloned.1.call-done) | copy-start | bytes 6291460
  305.9 108.2 %all-reduce.9.cloned.1.call-start = ((), (), s32[]{:S(2)}) async-start(), calls=%async_computation.2 | async-start | bytes 524288 | tf_op jit(solution)/shard_map/psum | solution.py:49
  378.4 35.7 %copy-start.8 = (f32[128,128]{1,0:T(8,128)S(1)}, f32[128,128]{1,0:T(8,128)}, u32[]{:S(2)}) copy-start(f32[128,128]{1,0:T(8,128)} %get-tuple-element.13) | copy-start | bytes 196612
  382.5 113.5 %all-reduce.15.cloned.1.call-start = ((), (), s32[]{:S(2)}) async-start(), calls=%async_computation.5 | async-start | bytes 1310720 | tf_op jit(solution)/shard_map/psum | solution.py:56
  415.5 2.0 copy-start.3
  421.8 135.4 %all-reduce.11.cloned.1.call-start = ((), (), s32[]{:S(2)}) async-start(), calls=%async_computation.3 | async-start | bytes 524288 | tf_op jit(solution)/shard_map/psum | solution.py:49
  525.3 112.7 %all-reduce.13.cloned.1.call-start = ((), (), s32[]{:S(2)}) async-start(), calls=%async_computation.4 | async-start | bytes 1310720 | tf_op jit(solution)/shard_map/psum | solution.py:65
  558.5 3.1 copy-start.4
  563.6 103.6 %copy-start.5 = (f32[512,128]{0,1:T(8,128)S(1)}, f32[512,128]{0,1:T(8,128)}, u32[]{:S(2)}) copy-start(f32[512,128]{0,1:T(8,128)} %copy-done.4) | copy-start | bytes 786436
  639.2 0.6 copy-start.7
  670.9 33.3 %copy-start.6 = (f32[512,128]{1,0:T(8,128)S(1)}, f32[512,128]{1,0:T(8,128)}, u32[]{:S(2)}) copy-start(f32[512,128]{1,0:T(8,128)} %fusion.18) | copy-start | bytes 786436
Sparse Core Ops, SparseCore 0:
  17.6 282.2 reduce-scatter.1
  306.0 72.3 all-reduce.16
  382.7 31.4 all-reduce.8
  421.9 74.0 all-reduce.14
  525.4 31.6 all-reduce.10
  563.7 74.1 all-reduce.12
where the time goes:
time: 721 us; the launch traced here: 714 us
  waiting for transfers between devices  563 us (78%)
  other arithmetic  76.7 us (11%)
  matrix products  51 us (7%)
  between operations  15.7 us (2%)
    reduce_scatter x1, waiting for transfers between devices, shards(): lax.psum_scatter(lax.dot_general(tokens, cotangent, (((0,), (0,)), ((), (...  280 us
    psum x1, waiting for transfers between devices, shards(): lax.psum((product(previous.T, applied), product(applied.T, applied), prod...  74.3 us
    psum x1, waiting for transfers between devices, shards(): lax.psum((product(applied.T, applied), product(sketch.T, applied), produc...  74.2 us
    psum x1, waiting for transfers between devices, shards(): lax.psum((product(sketch.T, sketch), product(gradient.T, sketch)), 'dp')  72.5 us
    psum x2, waiting for transfers between devices, covariance(): summed = lax.psum(partial_cols, 'mp')  61.6 us
    dot_general x13, matrix products, product(): return jnp.dot(left_mat, right_mat, precision=lax.Precision.HIGHEST)  31.1 us
    another operation x4, other arithmetic, right_solve(): lax.linalg.triangular_solve(lower_tri, values, left_side=False, lower=Tru...  20.9 us
  transfers between devices with their start and end apart: 6, of which 6 were waited for; matrix products, arithmetic and copies ran while one was open for 0% of the time, Pallas kernels for 0%

commit v1 on v0

--- a/solution.py
+++ b/solution.py
@@ -46,7 +46,10 @@
 
     def covariance(sketch_proj, grad_proj):
         partial_cols = product(gradient, grad_proj)
-        summed = lax.psum(partial_cols, "mp")
+        _turn_map = lambda local_values: jnp.sum(
+            lax.all_gather(local_values, axis_name="mp"), axis=0
+        )
+        summed = _turn_map(partial_cols)
         return DECAY_RATE * product(sketch, sketch_proj) + summed
 
     sketch_proj, grad_proj = lax.psum(

time: 721 us -> 697 us (0.967)
  waiting for transfers between devices: 563 us -> 532 us
    psum x2 -> x0, waiting for transfers between devices: 61.6 us -> none  [covariance(): summed = lax.psum(partial_cols, 'mp')]
    all_gather x0 -> x2, waiting for transfers between devices: none -> 30.4 us  [covariance(): lax.all_gather(local_values, axis_name='mp')]
where the time goes in v1:
time: 697 us; the launch traced here: 689 us
  waiting for transfers between devices  532 us (76%)
  other arithmetic  81.3 us (12%)
  matrix products  50 us (7%)
  between operations  15.7 us (2%)
  local copies, waits for them, and re-layouts  9.79 us (1%)
    reduce_scatter x1, waiting for transfers between devices, shards(): lax.psum_scatter(lax.dot_general(tokens, cotangent, (((0,), (0,)), ((), (...  280 us
    psum x1, waiting for transfers between devices, shards(): lax.psum((product(previous.T, applied), product(applied.T, applied), prod...  74.3 us
    psum x1, waiting for transfers between devices, shards(): lax.psum((product(applied.T, applied), product(sketch.T, applied), produc...  74.2 us
    psum x1, waiting for transfers between devices, shards(): lax.psum((product(sketch.T, sketch), product(gradient.T, sketch)), 'dp')  72.5 us
    all_gather x2, waiting for transfers between devices, covariance(): lax.all_gather(local_values, axis_name='mp')  30.4 us
    dot_general x13, matrix products, product(): return jnp.dot(left_mat, right_mat, precision=lax.Precision.HIGHEST)  30.1 us
    another operation x4, other arithmetic, right_solve(): lax.linalg.triangular_solve(lower_tri, values, left_side=False, lower=Tru...  22.4 us
  transfers between devices with their start and end apart: 6, of which 6 were waited for; matrix products, arithmetic and copies ran while one was open for 0% of the time, Pallas kernels for 0%

profile of v1, /device:TPU:0, one launch (start us, length us, event | category | flops | bytes accessed | tf_op | source)
XLA Modules:
  0.0 689.5 jit_solution(3854036273949587520)
XLA Ops:
  7.2 1.2 copy-done
  8.4 9.0 %convolution_multiply_fusion = f32[4096,1024]{1,0:T(8,128)} fusion(bf16[128,4096]{1,0:T(8,128)(2,1)S(1)} %copy-done, bf16[128,1024]{1,0:T(8,128)(2,1)} %param.11), kind=kOutput, calls=%fused_computation | convolution fusion | flops 1077936128 | bytes 18087936 | tf_op jit(solution)/shard_map/dot_general | solution.py:37
  17.5 0.9 copy-done.2
  18.4 1.2 fusion.33
  19.6 280.3 %reduce-scatter.2.cloned.1.call-done = f32[512,1024]{1,0:T(8,128)} async-done(((f32[4096,1024]{1,0:T(8,128)}), f32[512,1024]{1,0:T(8,128)}) %reduce-scatter.2.cloned.1.call-update) | async-done | bytes 2097168 | tf_op jit(solution)/shard_map/reduce_scatter | solution.py:36
  299.9 6.0 fusion.34
  305.9 72.5 %all-reduce.11.cloned.1.call-done = (f32[1024,128]{1,0:T(8,128)}, f32[128,128]{1,0:T(8,128)}) async-done(((f32[1024,128]{1,0:T(8,128)}, f32[128,128]{1,0:T(8,128)}), (f32[1024,128]{1,0:T(8,128)}, f32[128,128]{1,0:T(8,128)})) %all-reduce.11.cloned.1.call-update) | async-done | bytes 589840 | tf_op jit(solution)/shard_map/psum | solution.py:55
  378.4 3.6 fusion.35
  382.6 15.5 %all-gather.5.cloned.1.call-done = f32[2048,128]{1,0:T(8,128)} async-done(((f32[512,128]{1,0:T(8,128)}), f32[2048,128]{1,0:T(8,128)}) %all-gather.5.cloned.1.call-update) | async-done | bytes 1048592 | tf_op jit(solution)/shard_map/all_gather | solution.py:50
  398.0 2.0 reduce_sum.28
  400.0 1.8 copy.13
  401.8 1.4 fusion.3
  403.2 1.0 convolution_bitcast_fusion.2
  404.2 1.0 fusion.36
  405.2 4.2 fusion.37
  409.5 74.2 %all-reduce.9.cloned.1.call-done = (f32[1024,128]{1,0:T(8,128)}, f32[128,128]{0,1:T(8,128)}, f32[128,128]{0,1:T(8,128)}) async-done(((f32[1024,128]{1,0:T(8,128)}, f32[128,128]{0,1:T(8,128)}, f32[128,128]{0,1:T(8,128)}), (f32[1024,128]{1,0:T(8,128)}, f32[128,128]{0,1:T(8,128)}, f32[128,128]{0,1:T(8,128)})) %all-reduce.9.cloned.1.call-update) | async-done | bytes 655376 | tf_op jit(solution)/shard_map/psum | solution.py:59
  483.7 0.9 copy.15
  484.6 0.9 fusion.27
  485.5 11.7 %cholesky.59 = f32[128,128]{1,0:T(8,128)S(1)} custom-call(f32[128,128]{1,0:T(8,128)S(1)} %fusion.27), custom_call_target="Cholesky" | custom-call | tf_op jit(solution)/shard_map/jit(cholesky)/cholesky | solution.py:63
  497.9 1.3 fusion.5
  499.2 10.6 %custom-call.26 = f32[1,128,128]{1,2,0:T(8,128)S(1)} custom-call(f32[1,128,128]{2,1,0:T(8,128)} %fusion.5), custom_call_target="InvertDiagBlocksLowerTriangular" | custom-call | tf_op jit(solution)/shard_map/triangular_solve/custom-call.0 | solution.py:16
  509.8 1.6 fusion.24
  511.4 2.5 fusion.38
  514.2 1.1 convolution_bitcast_fusion.1
  515.3 14.9 %all-gather.7.cloned.1.call-done = f32[2048,128]{1,0:T(8,128)} async-done(((f32[512,128]{1,0:T(8,128)}), f32[2048,128]{1,0:T(8,128)}) %all-gather.7.cloned.1.call-update) | async-done | bytes 1048592 | tf_op jit(solution)/shard_map/all_gather | solution.py:50
  530.2 2.0 reduce_sum.29
  532.2 1.8 copy.16
  534.0 1.3 fusion.1
  535.4 2.0 fusion.39
  537.4 1.0 fusion.40
  538.4 2.1 fusion.41
  540.5 74.3 %all-reduce.7.cloned.1.call-done = (f32[128,128]{1,0:T(8,128)}, f32[128,1024]{1,0:T(8,128)}, f32[128,128]{1,0:T(8,128)}) async-done(((f32[128,128]{1,0:T(8,128)}, f32[128,1024]{1,0:T(8,128)}, f32[128,128]{1,0:T(8,128)}), (f32[128,128]{1,0:T(8,128)}, f32[128,1024]{1,0:T(8,128)}, f32[128,128]{1,0:T(8,128)})) %all-reduce.7.cloned.1.call-update) | async-done | bytes 655376 | tf_op jit(solution)/shard_map/psum | solution.py:68
  614.8 1.1 fusion.22
  617.3 0.9 fusion.32
  618.1 0.7 copy.18
  618.9 0.8 fusion.20
  619.8 11.7 %cholesky.70 = f32[128,128]{1,0:T(8,128)S(1)} custom-call(f32[128,128]{1,0:T(8,128)S(1)} %copy.19), custom_call_target="Cholesky" | custom-call | tf_op jit(solution)/shard_map/jit(cholesky)/cholesky | solution.py:75
  632.9 9.8 %custom-call.21 = f32[1,128,128]{1,2,0:T(8,128)S(1)} custom-call(f32[1,128,128]{2,1,0:T(8,128)S(1)} %fusion.6), custom_call_target="InvertDiagBlocksLowerTriangular" | custom-call | tf_op jit(solution)/shard_map/triangular_solve | solution.py:16
  642.7 1.3 fusion.18
  644.0 1.8 fusion.15
  646.3 1.1 fusion.4
  648.1 1.5 fusion.12
  649.6 1.6 copy.22
  651.2 12.7 %cholesky.81 = f32[128,128]{1,0:T(8,128)S(1)} custom-call(f32[128,128]{1,0:T(8,128)} %copy.22), custom_call_target="Cholesky" | custom-call | tf_op jit(solution)/shard_map/jit(cholesky)/cholesky | solution.py:28
  664.7 1.3 fusion.7
  666.0 10.6 %custom-call.22 = f32[1,128,128]{1,2,0:T(8,128)S(1)} custom-call(f32[1,128,128]{2,1,0:T(8,128)} %fusion.7), custom_call_target="InvertDiagBlocksLowerTriangular" | custom-call | tf_op jit(solution)/shard_map/triangular_solve | solution.py:22
  676.7 1.7 fusion.13
  679.6 2.8 subtract_convert_fusion
  (41 shorter events, 6.5 us)
Async XLA Ops:
  7.2 1.2 copy-start
  7.2 292.7 %reduce-scatter.2.cloned.1.call-start = ((), (), s32[]{:S(2)}) async-start(), calls=%async_computation.1 | async-start | bytes 18874368 | tf_op jit(solution)/shard_map/reduce_scatter | solution.py:36
  17.4 0.9 copy-start.2
  17.5 361.0 %all-reduce.11.cloned.1.call-start = ((), (), s32[]{:S(2)}) async-start(), calls=%async_computation.6 | async-start | bytes 1179648 | tf_op jit(solution)/shard_map/psum | solution.py:55
  299.9 78.6 %copy-start.1 = (f32[512,1024]{1,0:T(8,128)S(1)}, f32[512,1024]{1,0:T(8,128)}, u32[]{:S(2)}) copy-start(f32[512,1024]{1,0:T(8,128)} %reduce-scatter.2.cloned.1.call-done) | copy-start | bytes 6291460
  305.9 92.1 %all-gather.5.cloned.1.call-start = ((), (), s32[]{:S(2)}) async-start(), calls=%async_computation.2 | async-start | bytes 1310720 | tf_op jit(solution)/shard_map/all_gather | solution.py:50
  378.4 23.4 %copy-start.8 = (f32[128,128]{1,0:T(8,128)S(1)}, f32[128,128]{1,0:T(8,128)}, u32[]{:S(2)}) copy-start(f32[128,128]{1,0:T(8,128)} %get-tuple-element.13) | copy-start | bytes 196612
  382.0 101.7 %all-reduce.9.cloned.1.call-start = ((), (), s32[]{:S(2)}) async-start(), calls=%async_computation.5 | async-start | bytes 1310720 | tf_op jit(solution)/shard_map/psum | solution.py:59
  403.2 2.0 copy-start.3
  409.5 120.8 %all-gather.7.cloned.1.call-start = ((), (), s32[]{:S(2)}) async-start(), calls=%async_computation.3 | async-start | bytes 1310720 | tf_op jit(solution)/shard_map/all_gather | solution.py:50
  514.0 100.9 %all-reduce.7.cloned.1.call-start = ((), (), s32[]{:S(2)}) async-start(), calls=%async_computation.4 | async-start | bytes 1310720 | tf_op jit(solution)/shard_map/psum | solution.py:68
  535.4 3.1 copy-start.4
  540.5 102.2 %copy-start.5 = (f32[512,128]{0,1:T(8,128)S(1)}, f32[512,128]{0,1:T(8,128)}, u32[]{:S(2)}) copy-start(f32[512,128]{0,1:T(8,128)} %copy-done.4) | copy-start | bytes 786436
  616.1 0.6 copy-start.7
  646.3 33.3 %copy-start.6 = (f32[512,128]{1,0:T(8,128)S(1)}, f32[512,128]{1,0:T(8,128)}, u32[]{:S(2)}) copy-start(f32[512,128]{1,0:T(8,128)} %fusion.18) | copy-start | bytes 786436
Sparse Core Ops, SparseCore 0:
  17.6 282.2 reduce-scatter.1
  306.0 72.3 all-reduce.10
  382.2 15.8 all-gather.4
  409.6 74.0 all-reduce.8
  514.1 16.0 all-gather.6
  540.6 74.1 all-reduce.6
